TPU v7x, 256 devices: a whole 4x4x8 slice. The times are simulated.
256 devices in a mesh: fsdp: 32 (over z_hi, y, core), tensor: 8 (over z_lo, x).
Axes of the slice: x: 4, y: 4, z: 8 (z_hi: 4, z_lo: 2; z = z_hi * 2 + z_lo), core: 2. Of those that a mesh axis runs over, the one named last changes fastest.
Arguments:
- tokens: bfloat16 [4096, 8192], P('fsdp'), may hold values from -6 to 6
- cotangent: bfloat16 [4096, 8192], P('fsdp'), may hold values from -1.5 to 1.5
- gate_blocks: bfloat16 [8, 64, 128, 128], P('tensor', 'fsdp'), may hold values from -0.25 to 0.25
- up_blocks: bfloat16 [8, 64, 128, 128], P('tensor', 'fsdp'), may hold values from -0.25 to 0.25
- down_blocks: bfloat16 [8, 64, 128, 128], P('tensor', 'fsdp'), may hold values from -0.25 to 0.25
- gate_where: int32 [8, 64], P('tensor'), may hold values from 0 to 895, as said below
- up_where: int32 [8, 64], P('tensor'), may hold values from 0 to 895, as said below
- down_where: int32 [8, 64], P('tensor'), may hold values from 0 to 895, as said below
- block_counts: int32 [3, 8], P(None, 'tensor'), may hold values from 32 to 64, as said below
Outputs:
- outputs: bfloat16 [4096, 8192], P('fsdp', 'tensor')
- input_grads: bfloat16 [4096, 8192], P('fsdp', 'tensor')
- gate_grads: bfloat16 [8, 64, 128, 128], P('tensor', 'fsdp')
- up_grads: bfloat16 [8, 64, 128, 128], P('tensor', 'fsdp')
- down_grads: bfloat16 [8, 64, 128, 128], P('tensor', 'fsdp')
Inputs may be any that keep to these rules, and one draw needn't show every extreme that they name: Within one group of hidden units the 64 positions of gate_where are distinct. Within one group of hidden units the 64 positions of up_where are distinct. Within one group of hidden units the 64 positions of down_where are distinct. `block_counts`: for each matrix some group has all 64 slots live.
All inputs are finite; a program needn't handle non-finite values.
Results may differ from a plain program's by a relative error of at most 0.015.
Values may be sent and summed in bfloat16 or wider, within the bound.
A program may use at most 128 MiB of HBM per device.

v0:
```python
import jax
import jax.numpy as jnp
from jax import lax
from jax.sharding import PartitionSpec as P

FF = 14336


def blockwise(pattern, left_side, right_side):
    return jnp.einsum(pattern, left_side, right_side, preferred_element_type=jnp.float32)


def collect(block_terms, segment_ids, segments):
    return jax.ops.segment_sum(block_terms, segment_ids, num_segments=segments)


def shards(
    tokens,
    cotangent,
    gate_blocks,
    up_blocks,
    down_blocks,
    gate_where,
    up_where,
    down_where,
    block_counts,
):
    tok_rows, tok_width = tokens.shape
    row_blocks = tok_width // 128
    col_blocks = FF // (128 * lax.axis_size("tensor"))
    slot_count = gate_where.shape[1]
    rows_blocked = tokens.reshape(tok_rows, row_blocks, 128).transpose(1, 0, 2)
    grad_blocked = cotangent.reshape(tok_rows, row_blocks, 128).transpose(1, 0, 2)
    live_slots = lax.broadcasted_iota(jnp.int32, (3, slot_count), 1) < block_counts
    live_blocks = live_slots.astype(jnp.bfloat16)[:, :, None, None]
    live_parts = live_slots.astype(jnp.float32)[:, :, None, None]
    gate_all, up_all, down_all = (
        lax.all_gather(gate_blocks, "fsdp", axis=1, tiled=True),
        lax.all_gather(up_blocks, "fsdp", axis=1, tiled=True),
        lax.all_gather(down_blocks, "fsdp", axis=1, tiled=True),
    )
    gate_eff = gate_all[0] * live_blocks[0]
    up_eff = up_all[0] * live_blocks[1]
    gate_row = gate_where[0] // col_blocks
    gate_col = gate_where[0] % col_blocks
    up_row = up_where[0] // col_blocks
    up_col = up_where[0] % col_blocks
    down_ff = down_where[0] // row_blocks
    down_d = down_where[0] % row_blocks
    rows_gate = jnp.take(rows_blocked, gate_row, axis=0)
    rows_up = jnp.take(rows_blocked, up_row, axis=0)
    gate_val = collect(blockwise("ntk,nkj->ntj", rows_gate, gate_eff), gate_col, col_blocks)
    up_val = collect(blockwise("ntk,nkj->ntj", rows_up, up_eff), up_col, col_blocks)
    down_eff = down_all[0] * live_blocks[2]
    gate_sig = jax.nn.sigmoid(gate_val)
    silu_gate = gate_val * gate_sig
    hidden = (silu_gate * up_val).astype(jnp.bfloat16)
    hidden_sel = jnp.take(hidden, down_ff, axis=0)
    grad_sel = jnp.take(grad_blocked, down_d, axis=0)
    output_term = collect(blockwise("ntk,nkj->ntj", hidden_sel, down_eff), down_d, row_blocks)
    output_sum = lax.psum_scatter(
        output_term.astype(jnp.bfloat16), "tensor", scatter_dimension=0, tiled=True
    ).astype(jnp.float32)
    hidden_grad = collect(blockwise("ntj,nkj->ntk", grad_sel, down_eff), down_ff, col_blocks)
    down_part = blockwise("ntk,ntj->nkj", hidden_sel, grad_sel) * live_parts[2]
    gate_delta = (hidden_grad * up_val * gate_sig * (1.0 + gate_val * (1.0 - gate_sig))).astype(
        jnp.bfloat16
    )
    up_delta = (hidden_grad * silu_gate).astype(jnp.bfloat16)
    delta_gate = jnp.take(gate_delta, gate_col, axis=0)
    delta_up = jnp.take(up_delta, up_col, axis=0)
    input_term = collect(blockwise("ntj,nkj->ntk", delta_gate, gate_eff), gate_row, row_blocks)
    input_term = input_term + collect(
        blockwise("ntj,nkj->ntk", delta_up, up_eff), up_row, row_blocks
    )
    gate_part = blockwise("ntk,ntj->nkj", rows_gate, delta_gate) * live_parts[0]
    up_part = blockwise("ntk,ntj->nkj", rows_up, delta_up) * live_parts[1]
    gate_sum, up_sum, down_sum = (
        lax.psum_scatter(
            gate_part[None].astype(jnp.bfloat16), "fsdp", scatter_dimension=1, tiled=True
        ).astype(jnp.float32),
        lax.psum_scatter(
            up_part[None].astype(jnp.bfloat16), "fsdp", scatter_dimension=1, tiled=True
        ).astype(jnp.float32),
        lax.psum_scatter(
            down_part[None].astype(jnp.bfloat16), "fsdp", scatter_dimension=1, tiled=True
        ).astype(jnp.float32),
    )
    input_sum = lax.psum_scatter(
        input_term.astype(jnp.bfloat16), "tensor", scatter_dimension=0, tiled=True
    ).astype(jnp.float32)
    outputs = output_sum.transpose(1, 0, 2).reshape(tok_rows, -1).astype(jnp.bfloat16)
    input_grads = input_sum.transpose(1, 0, 2).reshape(tok_rows, -1).astype(jnp.bfloat16)
    return (
        outputs,
        input_grads,
        gate_sum.astype(jnp.bfloat16),
        up_sum.astype(jnp.bfloat16),
        down_sum.astype(jnp.bfloat16),
    )


def solution(mesh):
    placed = (
        P("fsdp", None),
        P("fsdp", None),
        P("tensor", "fsdp", None, None),
        P("tensor", "fsdp", None, None),
        P("tensor", "fsdp", None, None),
        P("tensor", None),
        P("tensor", None),
        P("tensor", None),
        P(None, "tensor"),
    )
    return jax.shard_map(
        shards,
        mesh=mesh,
        in_specs=placed,
        out_specs=(
            P("fsdp", "tensor"),
            P("fsdp", "tensor"),
            P("tensor", "fsdp", None, None),
            P("tensor", "fsdp", None, None),
            P("tensor", "fsdp", None, None),
        ),
        check_vma=False,
    )
```

profile of v0, /device:TPU:1, one launch (start us, length us, event | category | flops | bytes accessed | tf_op | source)
XLA Modules:
  0.0 605.7 jit_solution(10214975213814710242)
XLA Ops:
  9.4 4.1 copy.31
  13.6 3.2 copy.32
  21.3 3.2 copy.37
  24.5 3.0 copy.38
  27.5 2.5 gather_fusion.3
  30.2 39.3 %all-gather.8.cloned.1.call-done = bf16[1,64,128,128]{3,2,0,1:T(8,128)(2,1)} async-done(((bf16[1,2,128,128]{3,2,0,1:T(8,128)(2,1)}), bf16[1,64,128,128]{3,2,0,1:T(8,128)(2,1)}) %all-gather.8.cloned.1.call-update) | async-done | bytes 2097168 | tf_op jit(solution)/shard_map/all_gather | solution.py:40
  69.5 5.2 fusion.4
  74.8 8.9 %scatter_fusion.3 = f32[14,128,128]{2,1,0:T(8,128)S(1)} fusion(f32[14,128,128]{2,1,0:T(8,128)S(1)} %broadcast.235.clone, s32[64]{0:T(128)S(1)} %get-tuple-element.50, f32[64,128,128]{2,1,0:T(8,128)} %fusion.4), kind=kCustom, calls=%fused_computation.9 | custom fusion | flops 1048576 | bytes 12583168 | tf_op jit(solution)/shard_map/scatter-add | solution.py:14
  83.7 40.1 %all-gather.4.cloned.1.call-done = bf16[1,64,128,128]{3,2,0,1:T(8,128)(2,1)} async-done(((bf16[1,2,128,128]{3,2,0,1:T(8,128)(2,1)}), bf16[1,64,128,128]{3,2,0,1:T(8,128)(2,1)}) %all-gather.4.cloned.1.call-update) | async-done | bytes 2097168 | tf_op jit(solution)/shard_map/all_gather | solution.py:38
  123.9 4.3 fusion.1
  128.3 8.8 %scatter_fusion = f32[14,128,128]{2,1,0:T(8,128)S(1)} fusion(f32[14,128,128]{2,1,0:T(8,128)S(1)} %broadcast.235.clone.1, s32[64]{0:T(128)S(1)} %get-tuple-element.52, f32[64,128,128]{2,1,0:T(8,128)} %fusion.1), kind=kCustom, calls=%fused_computation.6 | custom fusion | flops 1048576 | bytes 12583168 | tf_op jit(solution)/shard_map/scatter-add | solution.py:14
  137.1 41.1 %all-gather.6.cloned.1.call-done = bf16[1,64,128,128]{3,2,0,1:T(8,128)(2,1)} async-done(((bf16[1,2,128,128]{3,2,0,1:T(8,128)(2,1)}), bf16[1,64,128,128]{3,2,0,1:T(8,128)(2,1)}) %all-gather.6.cloned.1.call-update) | async-done | bytes 2097168 | tf_op jit(solution)/shard_map/all_gather | solution.py:39
  178.2 5.0 fusion.3
  183.3 8.8 %scatter_fusion.1 = f32[14,128,128]{2,1,0:T(8,128)S(1)} fusion(f32[14,128,128]{2,1,0:T(8,128)S(1)} %broadcast.235.clone.2, s32[64]{0:T(128)S(1)} %get-tuple-element.53, f32[64,128,128]{2,1,0:T(8,128)} %fusion.3), kind=kCustom, calls=%fused_computation.7 | custom fusion | flops 1048576 | bytes 12583168 | tf_op jit(solution)/shard_map/scatter-add | solution.py:14
  193.7 3.3 gather_fusion.2
  197.0 4.3 fusion.5
  201.4 2.5 broadcast.233.clone
  203.8 13.5 %scatter_fusion.2 = f32[64,128,128]{2,1,0:T(8,128)} fusion(f32[64,128,128]{2,1,0:T(8,128)} %broadcast.233.clone, s32[64]{0:T(128)S(1)} %get-tuple-element.51, f32[64,128,128]{2,1,0:T(8,128)} %fusion.5), kind=kCustom, calls=%fused_computation.8 | custom fusion | flops 1048576 | bytes 12583168 | tf_op jit(solution)/shard_map/scatter-add | solution.py:14
  217.4 3.9 convert_element_type.63
  226.7 5.2 fusion
  234.4 13.7 %scatter_fusion.4 = f32[64,128,128]{2,1,0:T(8,128)} fusion(f32[64,128,128]{2,1,0:T(8,128)} %broadcast.233.clone.1, s32[64]{0:T(128)S(1)} %get-tuple-element.25, f32[64,128,128]{2,1,0:T(8,128)} %fusion), kind=kCustom, calls=%fused_computation.10 | custom fusion | flops 1048576 | bytes 12583168 | tf_op jit(solution)/shard_map/scatter-add | solution.py:14
  248.1 5.2 fusion.2
  253.3 2.5 broadcast.233.clone.2
  255.8 13.6 %scatter_fusion.5 = f32[64,128,128]{2,1,0:T(8,128)} fusion(f32[64,128,128]{2,1,0:T(8,128)} %broadcast.233.clone.2, s32[64]{0:T(128)S(1)} %get-tuple-element.19, f32[64,128,128]{2,1,0:T(8,128)} %fusion.2), kind=kCustom, calls=%fused_computation.11 | custom fusion | flops 1048576 | bytes 12583168 | tf_op jit(solution)/shard_map/scatter-add | solution.py:14
  269.4 5.8 add_convert_fusion
  276.7 4.2 fusion.7
  282.5 4.3 fusion.6
  288.4 4.2 fusion.8
  294.6 17.7 %reduce-scatter.8.cloned.1.call-done = bf16[8,128,128]{2,1,0:T(8,128)(2,1)} async-done(((bf16[64,128,128]{2,1,0:T(8,128)(2,1)}), bf16[8,128,128]{2,1,0:T(8,128)(2,1)}) %reduce-scatter.8.cloned.1.call-update) | async-done | bytes 262160 | tf_op jit(solution)/shard_map/reduce_scatter | solution.py:89
  314.2 96.3 %reduce-scatter.12.cloned.1.call-done = bf16[1,2,128,128]{3,2,1,0:T(8,128)(2,1)} async-done(((bf16[1,64,128,128]{3,2,1,0:T(8,128)(2,1)}), bf16[1,2,128,128]{3,2,1,0:T(8,128)(2,1)}) %reduce-scatter.12.cloned.1.call-update) | async-done | bytes 65552 | tf_op jit(solution)/shard_map/reduce_scatter | solution.py:82
  410.6 94.1 %reduce-scatter.10.cloned.1.call-done = bf16[1,2,128,128]{3,2,1,0:T(8,128)(2,1)} async-done(((bf16[1,64,128,128]{3,2,1,0:T(8,128)(2,1)}), bf16[1,2,128,128]{3,2,1,0:T(8,128)(2,1)}) %reduce-scatter.10.cloned.1.call-update) | async-done | bytes 65552 | tf_op jit(solution)/shard_map/reduce_scatter | solution.py:79
  504.7 94.2 %reduce-scatter.14.cloned.1.call-done = bf16[1,2,128,128]{3,2,1,0:T(8,128)(2,1)} async-done(((bf16[1,64,128,128]{3,2,1,0:T(8,128)(2,1)}), bf16[1,2,128,128]{3,2,1,0:T(8,128)(2,1)}) %reduce-scatter.14.cloned.1.call-update) | async-done | bytes 65552 | tf_op jit(solution)/shard_map/reduce_scatter | solution.py:85
  (68 shorter events, 25.2 us)
Async XLA Ops:
  7.2 62.4 %all-gather.8.cloned.1.call-start = ((), (), s32[]{:S(2)}) async-start(), calls=%async_computation.7 | async-start | bytes 2162688 | tf_op jit(solution)/shard_map/all_gather | solution.py:40
  7.9 116.0 %all-gather.4.cloned.1.call-start = ((), (), s32[]{:S(2)}) async-start(), calls=%async_computation.5 | async-start | bytes 2162688 | tf_op jit(solution)/shard_map/all_gather | solution.py:38
  8.6 169.6 %all-gather.6.cloned.1.call-start = ((), (), s32[]{:S(2)}) async-start(), calls=%async_computation.6 | async-start | bytes 2162688 | tf_op jit(solution)/shard_map/all_gather | solution.py:39
  9.4 283.2 %reduce-scatter.6.cloned.1.call-start = ((), (), s32[]{:S(2)}) async-start(), calls=%async_computation.8 | async-start | bytes 2359296 | tf_op jit(solution)/shard_map/reduce_scatter | solution.py:61
  13.6 3.2 copy-start.9
  16.9 2.2 copy-start.10
  24.5 3.0 copy-start.11
  27.5 2.6 copy-start.12
  30.1 44.7 %copy-start.5 = (bf16[64,128,128]{2,1,0:T(8,128)(2,1)}, bf16[64,128,128]{2,1,0:T(8,128)(2,1)S(1)}, u32[]{:S(2)}) copy-start(bf16[64,128,128]{2,1,0:T(8,128)(2,1)S(1)} %gather_fusion.3) | copy-start | bytes 6291460
  74.8 49.1 %copy-start.7 = (bf16[64,128,128]{2,1,0:T(8,128)(2,1)S(1)}, bf16[64,128,128]{2,1,0:T(8,128)(2,1)}, u32[]{:S(2)}) copy-start(bf16[64,128,128]{2,1,0:T(8,128)(2,1)} %gather_fusion) | copy-start | bytes 6291460
  193.7 3.3 copy-start.3
  221.3 1.0 copy-start
  221.3 90.9 %reduce-scatter.8.cloned.1.call-start = ((), (), s32[]{:S(2)}) async-start(), calls=%async_computation.9 | async-start | bytes 2359296 | tf_op jit(solution)/shard_map/reduce_scatter | solution.py:89
  224.5 2.2 copy-start.1
  234.4 13.7 %copy-start.2 = (bf16[1,64,128,128]{3,2,0,1:T(8,128)(2,1)S(1)}, bf16[1,64,128,128]{3,2,0,1:T(8,128)(2,1)}, u32[]{:S(2)}) copy-start(bf16[1,64,128,128]{3,2,0,1:T(8,128)(2,1)} %all-gather.6.cloned.1.call-done) | copy-start | bytes 6291460
  275.1 1.6 copy-start.4
  275.1 135.4 %reduce-scatter.12.cloned.1.call-start = ((), (), s32[]{:S(2)}) async-start(), calls=%async_computation.11 | async-start | bytes 2162688 | tf_op jit(solution)/shard_map/reduce_scatter | solution.py:82
  280.9 1.6 copy-start.8
  280.9 223.8 %reduce-scatter.10.cloned.1.call-start = ((), (), s32[]{:S(2)}) async-start(), calls=%async_computation.10 | async-start | bytes 2162688 | tf_op jit(solution)/shard_map/reduce_scatter | solution.py:79
  286.8 1.6 copy-start.6
  286.8 312.0 %reduce-scatter.14.cloned.1.call-start = ((), (), s32[]{:S(2)}) async-start(), calls=%async_computation.12 | async-start | bytes 2162688 | tf_op jit(solution)/shard_map/reduce_scatter | solution.py:85
Sparse Core Ops, SparseCore 0:
  10.5 58.9 all-gather.7
  72.1 51.7 all-gather.3
  126.4 51.7 all-gather.5
  221.4 37.0 reduce-scatter.5
  275.3 36.9 reduce-scatter.7
  316.5 94.0 reduce-scatter.11
  415.0 89.6 reduce-scatter.9
  509.1 89.7 reduce-scatter.13
where the time goes:
time: 608 us; the launch traced here: 606 us
  waiting for transfers between devices  425 us (70%)
  other arithmetic  78.8 us (13%)
  local copies, waits for them, and re-layouts  45.1 us (7%)
  matrix products  42 us (7%)
  between operations  14.4 us (2%)
    reduce_scatter x1, waiting for transfers between devices, shards(): lax.psum_scatter(up_part[None].astype(jnp.bfloat16), 'fsdp', scatter_dime...  96.3 us
    reduce_scatter x1, waiting for transfers between devices, shards(): lax.psum_scatter(down_part[None].astype(jnp.bfloat16), 'fsdp', scatter_di...  94.2 us
    reduce_scatter x1, waiting for transfers between devices, shards(): lax.psum_scatter(gate_part[None].astype(jnp.bfloat16), 'fsdp', scatter_di...  94.1 us
    scatter-add x6, other arithmetic, collect(): return jax.ops.segment_sum(block_terms, segment_ids, num_segments=segments)  67.3 us
    dot_general x9, matrix products, blockwise(): jnp.einsum(pattern, left_side, right_side, preferred_element_type=jnp.flo...  42 us
    all_gather x1, waiting for transfers between devices, shards(): lax.all_gather(up_blocks, 'fsdp', axis=1, tiled=True)  41.1 us
    all_gather x1, waiting for transfers between devices, shards(): lax.all_gather(gate_blocks, 'fsdp', axis=1, tiled=True)  40.1 us
    all_gather x1, waiting for transfers between devices, shards(): lax.all_gather(down_blocks, 'fsdp', axis=1, tiled=True)  39.3 us
  transfers between devices with their start and end apart: 8, of which 7 were waited for; matrix products, arithmetic and copies ran while one was open for 19% of the time, Pallas kernels for 0%

commit v1 on v0

v1 whole, which is shorter than its diff:
```python
import jax
import jax.numpy as jnp
from jax import lax
from jax.experimental import pallas as pl
from jax.experimental.pallas import tpu as pltpu
from jax.sharding import PartitionSpec as P

FF = 14336
BK = 128
BF = jnp.bfloat16
F32 = jnp.float32
MESH = pl.DeviceIdType.MESH
VM = pl.BlockSpec(memory_space=pltpu.VMEM)
SM = pl.BlockSpec(memory_space=pltpu.SMEM)
ANY = pl.BlockSpec(memory_space=pl.ANY)
NZ, NY = 4, 4
HALF = (slice(0, 3), slice(3, 6))


class Place:
    def __init__(self):
        rem, div = lax.rem, lax.div
        self.f = lax.axis_index("fsdp")
        self.t = lax.axis_index("tensor")
        self.c = rem(self.f, 2)
        chip = div(self.f, 2)
        y, zh = rem(chip, 4), div(chip, 4)
        self.zl = div(self.t, 4)
        x = rem(self.t, 4)
        self.ys = [rem(y + j, 4) for j in range(4)]
        self.zs = [rem(zh + k, 4) for k in range(4)]
        self.xs = [rem(x + m, 4) for m in range(4)]
        self.same = [[(self.zs[k] * 4 + self.ys[j]) * 2 + self.c for j in range(4)] for k in range(4)]
        self.twin = [[(self.zs[k] * 4 + self.ys[j]) * 2 + (1 - self.c) for j in range(4)] for k in range(4)]
        self.line = [self.zl * 4 + v for v in self.xs]
        self.across = (1 - self.zl) * 4 + x

    def fs(self, k=0, j=0):
        return self.same[k % 4][j % 4]

    def dev(self, k=0, j=0, flip=False):
        return ((self.twin if flip else self.same)[k % 4][j % 4], self.t)

    def tdev(self, m=0, flip=False):
        return (self.f, self.across if flip else self.line[m % 4])


class Sender:
    def __init__(self, sems):
        self.sems = sems
        self.sent = []

    def __call__(self, src, dst, recv, dev):
        copy = pltpu.make_async_remote_copy(
            src_ref=src,
            dst_ref=dst,
            send_sem=self.sems.at[len(self.sent)],
            recv_sem=recv,
            device_id=dev,
            device_id_type=MESH,
        )
        copy.start()
        self.sent.append(copy)

    def finish(self):
        for copy in self.sent:
            copy.wait_send()


def arrive(ref, sem):
    pltpu.make_async_copy(ref, ref, sem).wait()


def meet(devs):
    barrier = pltpu.get_barrier_semaphore()
    for dev in devs:
        pl.semaphore_signal(barrier, inc=1, device_id=dev, device_id_type=MESH)
    pl.semaphore_wait(barrier, len(devs))


ORDER, KEEP, END, SOME = 0, 5, 10, 15
GR, GC, UR, UC, DF, DD = range(20, 26)
GATE, UP, HID, OUT, INP = range(5)
UNROLL = 8
SLOTS = 64
FLOWS = ((0, 2), (4, 1))


def half(fl, h, base=0):
    first, size = FLOWS[fl]
    return pl.ds(base + first + size * h, size)


def whole(fl):
    first, size = FLOWS[fl]
    return pl.ds(first, 2 * size)


def dot_nn(a, b):
    return lax.dot_general(a, b, (((1,), (0,)), ((), ())), preferred_element_type=F32)


def dot_nt(a, b):
    return lax.dot_general(a, b, (((1,), (1,)), ((), ())), preferred_element_type=F32)


def dot_tn(a, b):
    return lax.dot_general(a, b, (((0,), (0,)), ((), ())), preferred_element_type=F32)


def split14(v):
    q = (v * 4682) >> 16
    return q, v - q * 14


def table_kernel(counts, gw, uw, dw, tab):
    n64 = lax.broadcasted_iota(jnp.int32, (1, SLOTS), 1)
    gr, gc = split14(gw[...])
    ur, uc = split14(uw[...])
    df, dd = dw[...] >> 6, dw[...] & 63
    base = (n64 >> 1) * 6 + (n64 & 1)

    def key(k, v):
        return jnp.where(n64 < counts[k], v, 64)

    def wide(v, fill):
        return jnp.concatenate([v, jnp.full((1, SLOTS), fill, jnp.int32)], axis=1)

    keys = (
        wide(key(0, gc), 65),
        wide(key(1, uc), 65),
        wide(key(2, df), 65),
        wide(key(2, dd), 65),
        jnp.concatenate([key(0, gr), key(1, ur)], axis=1),
    )
    loads = (
        wide(n64, 0),
        wide(n64, 0),
        wide(n64, 0),
        wide((base + 4) * 64 + df, 0),
        jnp.concatenate([base * 64 + gc, (base + 2) * 64 + uc + 14], axis=1),
    )
    row_i = lax.broadcasted_iota(jnp.int32, (BK, BK), 0)
    col_i = lax.broadcasted_iota(jnp.int32, (BK, BK), 1)
    lane = lax.broadcasted_iota(jnp.int32, (1, BK), 1)
    for k in range(5):
        by_lane = jnp.broadcast_to(keys[k], (BK, BK))
        by_row = by_lane.T
        code = jnp.broadcast_to(loads[k] * 128 + keys[k], (BK, BK)).T
        before = (by_row < by_lane) | ((by_row == by_lane) & (row_i < col_i))
        rank = jnp.sum(before.astype(jnp.int32), axis=0, keepdims=True)
        rank_row = jnp.broadcast_to(rank, (BK, BK)).T
        both = jnp.sum(jnp.where(rank_row == col_i, code, 0), axis=0, keepdims=True)
        skey = both & 127
        tab[ORDER + k : ORDER + k + 1, :] = both >> 7
        same = (skey == pltpu.roll(skey, 1, 1)) & (lane > 0)
        tab[KEEP + k : KEEP + k + 1, :] = same.astype(jnp.int32)
        upto = jnp.sum((by_row <= col_i).astype(jnp.int32), axis=0, keepdims=True)
        some = jnp.sum((by_row == col_i).astype(jnp.int32), axis=0, keepdims=True)
        tab[END + k : END + k + 1, :] = jnp.maximum(upto - 1, 0)
        tab[SOME + k : SOME + k + 1, :] = (some > 0).astype(jnp.int32)
    for i, v in enumerate((gr, gc, ur, uc, df, dd)):
        tab[GR + i : GR + i + 1, :] = wide(v, 0)


def add2(a, b):
    return (a.astype(F32) + b.astype(F32)).astype(BF)


def add3(a, b, c):
    return a.astype(F32) + b.astype(F32) + c.astype(F32)


def layer_kernel(
    cnt, tab, x_hbm, g_hbm, gate_hbm, up_hbm, down_hbm,
    out_hbm, ing_hbm, gg_hbm, ug_hbm, dg_hbm,
    x, g, w, p, s, hid, delta,
    o, d, pbuf, y2, yr, bbuf, z2, zr, x2, xr, tz, zlb, fin, fing,
    lsem, fsem, ssem, rz, ry, rp, rq, ry2, ryr, rz2, rzr, rx2, rxr, rl,
):
    me = Place()
    own = me.fs()
    cols = hid.shape[0]
    local = [
        pltpu.make_async_copy(src.at[0], w.at[pl.ds(own * 6 + 2 * i, 2)], lsem.at[i])
        for i, src in enumerate((gate_hbm, up_hbm, down_hbm))
    ]
    for copy in local:
        copy.start()

    def bring(b, _):
        at = pl.ds(pl.multiple_of(b * BK, BK), BK)
        pltpu.make_async_copy(x_hbm.at[:, at], x.at[b], lsem.at[3]).start()
        pltpu.make_async_copy(g_hbm.at[:, at], g.at[b], lsem.at[4]).start()
        return 0

    lax.fori_loop(0, x.shape[0], bring, 0)
    meet([me.dev(1), me.dev(3), me.dev(0, 1), me.dev(0, 3), me.dev(flip=True),
          me.tdev(1), me.tdev(3), me.tdev(flip=True)])
    for copy in local:
        copy.wait()
    send = Sender(ssem)

    def piece(k, j, fl, h):
        return w.at[half(fl, h, me.fs(k, j) * 6)]

    def to_z(k, fl, h, step):
        send(piece(k, 0, fl, h), piece(k, 0, fl, h), rz.at[fl, (k - step) % 4, h], me.dev(step))

    def to_y(k, j, fl, h, step):
        send(piece(k, j, fl, h), piece(k, j, fl, h), ry.at[fl, k, (j - step) % 4, h], me.dev(0, step))

    def to_core(k, j, fl, h):
        send(piece(k, j, fl, h), piece(k, j, fl, h), rp.at[fl, k, j, h], me.dev(flip=True))

    def on_y(k, j, fl):
        for h in (0, 1):
            arrive(piece(k, j, fl, h), ry.at[fl, k, j, h])
            if j == 3 and h == 0:
                to_y(k, j, fl, h, 1)
            if j == 1 and h == 1:
                to_y(k, j, fl, h, -1)
            to_core(k, j, fl, h)

    def on_z(k, fl):
        for h in (0, 1):
            arrive(piece(k, 0, fl, h), rz.at[fl, k, h])
            if k == 3 and h == 0:
                to_z(k, fl, h, 1)
            if k == 1 and h == 1:
                to_z(k, fl, h, -1)
            to_y(k, 0, fl, h, 1)
            to_y(k, 0, fl, h, -1)
            to_core(k, 0, fl, h)

    def begin(fl):
        for h in (0, 1):
            to_z(0, fl, h, 1)
            to_z(0, fl, h, -1)
            to_y(0, 0, fl, h, 1)
            to_y(0, 0, fl, h, -1)
            to_core(0, 0, fl, h)

    def products(f, fl):
        for slot in (0, 1):
            n = 2 * f + slot
            if fl == 0:
                p[n] = dot_nn(x[tab[GR, n]], w[f * 6 + slot])
                p[SLOTS + n] = dot_nn(x[tab[UR, n]], w[f * 6 + 2 + slot])
            else:
                p[2 * SLOTS + n] = dot_nt(g[tab[DD, n]], w[f * 6 + 4 + slot])

    def mine(chunks, fl):
        for k, j in chunks:
            products(me.fs(k, j), fl)

    def theirs(chunks, fl):
        for k, j in chunks:
            f = me.twin[k][j]
            for h in (0, 1):
                arrive(w.at[half(fl, h, f * 6)], rp.at[fl, k, j, h])
        for k, j in chunks:
            products(me.twin[k][j], fl)

    groups = (
        ((0, 0),),
        ((0, 3), (0, 1), (3, 0), (1, 0)),
        ((2, 0), (0, 2)),
        ((3, 3), (3, 1), (1, 3), (1, 1)),
        ((3, 2), (1, 2)),
        ((2, 3), (2, 1)),
        ((2, 2),),
    )

    def take(i, fl):
        for k, j in groups[i]:
            if j == 0:
                on_z(k, fl)
            else:
                on_y(k, j, fl)

    def run(kind, count, first, term):
        def body(step, acc):
            for u in range(UNROLL):
                i = step * UNROLL + u
                keep = tab[KEEP + kind, i].astype(F32)
                acc = acc * keep + term(tab[ORDER + kind, i])
                s[first + i] = acc
            return acc

        lax.fori_loop(0, count // UNROLL, body, jnp.zeros((BK, BK), F32))

    def pick(first, kind, c):
        return s[first + tab[END + kind, c]] * tab[SOME + kind, c].astype(F32)

    begin(0)
    arrive(x, lsem.at[3])
    arrive(g, lsem.at[4])
    mine(groups[0], 0)
    for i in range(1, 7):
        take(i, 0)
        if i == 4:
            begin(1)
        mine(groups[i], 0)
        theirs(groups[i - 1], 0)
    mine(groups[0], 1)
    take(1, 1)
    theirs(groups[6], 0)
    run(GATE, SLOTS, 0, lambda n: p[n])
    take(2, 1)
    take(3, 1)
    run(UP, SLOTS, SLOTS, lambda n: p[SLOTS + n])
    mine(groups[1], 1)
    theirs(groups[0], 1)
    take(4, 1)

    def act(c, _):
        gate = pick(0, GATE, c)
        up = pick(SLOTS, UP, c)
        sig = jax.nn.sigmoid(gate)
        silu = gate * sig
        hid[c] = (silu * up).astype(BF)
        p[c] = up * sig * (1.0 + gate * (1.0 - sig))
        p[cols + c] = silu
        return 0

    lax.fori_loop(0, cols, act, 0)
    take(5, 1)
    mine(groups[2] + groups[3], 1)
    theirs(groups[1], 1)
    take(6, 1)
    mine(groups[4] + groups[5] + groups[6], 1)
    theirs(groups[2] + groups[3], 1)
    theirs(groups[4] + groups[5] + groups[6], 1)

    def opiece(a, zl, m):
        return o.at[a, zl * 4 + me.xs[m % 4]]

    def put(a, first, kind):
        def body(q, _):
            for r in range(8):
                o[a, q, :, r * BK : (r + 1) * BK] = pick(first, kind, q * 8 + r).astype(BF)
            return 0

        lax.fori_loop(0, 8, body, 0)

    def x_start(a):
        send(opiece(a, 0, 2), x2.at[a, 0], rx2.at[a, 0], me.tdev(1))
        send(opiece(a, 1, 2), x2.at[a, 1], rx2.at[a, 1], me.tdev(-1))
        send(opiece(a, 1, 1), xr.at[a, 0, 1], rxr.at[a, 0, 1], me.tdev(1))
        send(opiece(a, 0, -1), xr.at[a, 1, 0], rxr.at[a, 1, 0], me.tdev(-1))

    def x_pass(a):
        for h, m in ((0, 1), (1, -1)):
            arrive(x2.at[a, h], rx2.at[a, h])
            x2[a, h] = add2(o[a, h * 4 + me.xs[m % 4]], x2[a, h])
            send(x2.at[a, h], xr.at[a, h, h], rxr.at[a, h, h], me.tdev(m))

    def x_end(a):
        for e in (0, 1):
            for h in (0, 1):
                arrive(xr.at[a, e, h], rxr.at[a, e, h])
        other = 1 - me.zl
        tz[a] = add3(o[a, me.across], xr[a, 0, other], xr[a, 1, other]).astype(BF)
        send(tz.at[a], zlb.at[a], rl.at[a], me.tdev(flip=True))

    results = []

    def result(src, dst):
        copy = pltpu.make_async_copy(src, dst, fsem.at[len(results)])
        copy.start()
        results.append(copy)

    def l_end(a):
        own_sum = add3(o[a, me.line[0]], xr[a, 0, me.zl], xr[a, 1, me.zl])
        arrive(zlb.at[a], rl.at[a])
        fin[a] = (own_sum + zlb[a].astype(F32)).astype(BF)
        result(fin.at[a], (out_hbm, ing_hbm)[a])

    def core_send(k, fl):
        for j in (2, 1, 3, 0):
            send(d.at[me.twin[k][j], whole(fl)], pbuf.at[k, j, whole(fl)], rq.at[fl, k, j], me.dev(flip=True))

    def core_sum(k, j, fl):
        arrive(pbuf.at[k, j, whole(fl)], rq.at[fl, k, j])
        f = me.fs(k, j)
        d[f, whole(fl)] = add2(d[f, whole(fl)], pbuf[k, j, whole(fl)])

    def y_start(k, fl):
        core_sum(k, 2, fl)
        far = me.fs(k, 2)
        send(d.at[far, half(fl, 0)], y2.at[k, half(fl, 0)], ry2.at[fl, k, 0], me.dev(0, 1))
        send(d.at[far, half(fl, 1)], y2.at[k, half(fl, 1)], ry2.at[fl, k, 1], me.dev(0, -1))
        core_sum(k, 1, fl)
        send(d.at[me.fs(k, 1), half(fl, 1)], yr.at[k, 0, half(fl, 1)], ryr.at[fl, k, 0, 1], me.dev(0, 1))
        core_sum(k, 3, fl)
        send(d.at[me.fs(k, 3), half(fl, 0)], yr.at[k, 1, half(fl, 0)], ryr.at[fl, k, 1, 0], me.dev(0, -1))
        core_sum(k, 0, fl)

    def y_pass(k, fl):
        for h, j in ((0, 1), (1, 3)):
            at = half(fl, h)
            arrive(y2.at[k, at], ry2.at[fl, k, h])
            y2[k, at] = add2(d[me.fs(k, j), at], y2[k, at])
            send(y2.at[k, at], yr.at[k, h, at], ryr.at[fl, k, h, h], me.dev(0, j))

    def y_end(k, fl):
        for e in (0, 1):
            for h in (0, 1):
                arrive(yr.at[k, e, half(fl, h)], ryr.at[fl, k, e, h])
        at = whole(fl)
        bbuf[k, at] = add3(d[me.fs(k, 0), at], yr[k, 0, at], yr[k, 1, at]).astype(BF)
        if k == 2:
            send(bbuf.at[2, half(fl, 0)], z2.at[half(fl, 0)], rz2.at[fl, 0], me.dev(1))
            send(bbuf.at[2, half(fl, 1)], z2.at[half(fl, 1)], rz2.at[fl, 1], me.dev(-1))
        if k == 1:
            send(bbuf.at[1, half(fl, 1)], zr.at[0, half(fl, 1)], rzr.at[fl, 0, 1], me.dev(1))
        if k == 3:
            send(bbuf.at[3, half(fl, 0)], zr.at[1, half(fl, 0)], rzr.at[fl, 1, 0], me.dev(-1))

    def z_pass(fl):
        for h, k in ((0, 1), (1, 3)):
            at = half(fl, h)
            arrive(z2.at[at], rz2.at[fl, h])
            z2[at] = add2(bbuf[k, at], z2[at])
            send(z2.at[at], zr.at[h, at], rzr.at[fl, h, h], me.dev(k))

    def z_end(fl):
        for e in (0, 1):
            for h in (0, 1):
                arrive(zr.at[e, half(fl, h)], rzr.at[fl, e, h])
        at = whole(fl)
        fing[at] = add3(bbuf[0, at], zr[0, at], zr[1, at]).astype(BF)
        for b in (0, 1) if fl == 0 else (2,):
            result(fing.at[pl.ds(2 * b, 2)], (gg_hbm, ug_hbm, dg_hbm)[b].at[0])

    def live(k, n):
        return (n < cnt[k]).astype(F32)

    def down_grads(f, _):
        for slot in (0, 1):
            n = 2 * f + slot
            d[f, 4 + slot] = (dot_tn(hid[tab[DF, n]], g[tab[DD, n]]) * live(2, n)).astype(BF)
        return 0

    def in_grads(k):
        def body(i, _):
            f = me.zs[k] * 8 + i
            for slot in (0, 1):
                n = 2 * f + slot
                d[f, slot] = (dot_tn(x[tab[GR, n]], delta[tab[GC, n]]) * live(0, n)).astype(BF)
                d[f, 2 + slot] = (dot_tn(x[tab[UR, n]], delta[cols + tab[UC, n]]) * live(1, n)).astype(BF)
            return 0

        lax.fori_loop(0, 8, body, 0)
        core_send(k, 0)

    run(OUT, SLOTS, 0, lambda v: dot_nn(hid[v & 63], w[v >> 6]))
    put(0, 0, OUT)
    x_start(0)
    lax.fori_loop(0, 32, down_grads, 0)
    for k in (2, 1, 3, 0):
        core_send(k, 1)
    run(HID, SLOTS, 2 * SLOTS, lambda n: p[2 * SLOTS + n])

    def act_grad(c, _):
        hg = pick(2 * SLOTS, HID, c)
        delta[c] = (hg * p[c]).astype(BF)
        delta[cols + c] = (hg * p[cols + c]).astype(BF)
        return 0

    lax.fori_loop(0, cols, act_grad, 0)
    for k in (2, 1, 3, 0):
        y_start(k, 1)
    run(INP, 2 * SLOTS, SLOTS, lambda v: dot_nt(delta[v & 63], w[v >> 6]))
    put(1, SLOTS, INP)
    x_start(1)
    in_grads(2)
    x_pass(0)
    in_grads(1)
    y_start(2, 0)
    in_grads(3)
    y_start(1, 0)
    in_grads(0)
    y_start(3, 0)
    for k in (2, 1, 3, 0):
        y_pass(k, 1)
    y_start(0, 0)
    for k in (2, 1, 3, 0):
        y_end(k, 1)
    y_pass(2, 0)
    z_pass(1)
    x_end(0)
    y_pass(1, 0)
    y_pass(3, 0)
    y_end(2, 0)
    x_pass(1)
    y_pass(0, 0)
    y_end(1, 0)
    z_end(1)
    l_end(0)
    y_end(3, 0)
    z_pass(0)
    y_end(0, 0)
    x_end(1)
    z_end(0)
    l_end(1)
    for copy in results:
        copy.wait()
    send.finish()


def finish_kernel(*refs):
    for src, dst in zip(refs[:5], refs[5:]):
        dst[...] = src[...]


def shards(tokens, cotangent, gate_blocks, up_blocks, down_blocks, gate_where, up_where, down_where, block_counts):
    cols = FF // (BK * lax.axis_size("tensor"))
    toks = tokens.shape[0]
    dma = pltpu.SemaphoreType.DMA
    shapes = (
        jax.ShapeDtypeStruct((toks, 1024), BF),
        jax.ShapeDtypeStruct((toks, 1024), BF),
        jax.ShapeDtypeStruct((1, 2, BK, BK), BF),
        jax.ShapeDtypeStruct((1, 2, BK, BK), BF),
        jax.ShapeDtypeStruct((1, 2, BK, BK), BF),
    )
    counts = block_counts.reshape(3)
    table = pl.pallas_call(
        table_kernel,
        out_shape=jax.ShapeDtypeStruct((26, BK), jnp.int32),
        in_specs=[SM, VM, VM, VM],
        out_specs=VM,
    )(counts, gate_where, up_where, down_where)
    results = pl.pallas_call(
        layer_kernel,
        out_shape=shapes,
        in_specs=[SM, SM] + [ANY] * 5,
        out_specs=(ANY,) * 5,
        scratch_shapes=[
            pltpu.VMEM((tokens.shape[1] // BK, toks, BK), BF),
            pltpu.VMEM((tokens.shape[1] // BK, toks, BK), BF),
            pltpu.VMEM((192, BK, BK), BF),
            pltpu.VMEM((3 * SLOTS, BK, BK), F32),
            pltpu.VMEM((3 * SLOTS, BK, BK), F32),
            pltpu.VMEM((cols, BK, BK), BF),
            pltpu.VMEM((2 * cols, BK, BK), BF),
            pltpu.VMEM((2, 8, toks, 1024), BF),
            pltpu.VMEM((32, 6, BK, BK), BF),
            pltpu.VMEM((4, 4, 6, BK, BK), BF),
            pltpu.VMEM((4, 6, BK, BK), BF),
            pltpu.VMEM((4, 2, 6, BK, BK), BF),
            pltpu.VMEM((4, 6, BK, BK), BF),
            pltpu.VMEM((6, BK, BK), BF),
            pltpu.VMEM((2, 6, BK, BK), BF),
            pltpu.VMEM((2, 2, toks, 1024), BF),
            pltpu.VMEM((2, 2, 2, toks, 1024), BF),
            pltpu.VMEM((2, toks, 1024), BF),
            pltpu.VMEM((2, toks, 1024), BF),
            pltpu.VMEM((2, toks, 1024), BF),
            pltpu.VMEM((6, BK, BK), BF),
            dma((5,)),
            dma((5,)),
            dma((240,)),
            dma((2, 4, 2)),
            dma((2, 4, 4, 2)),
            dma((2, 4, 4, 2)),
            dma((2, 4, 4)),
            dma((2, 4, 2)),
            dma((2, 4, 2, 2)),
            dma((2, 2)),
            dma((2, 2, 2)),
            dma((2, 2)),
            dma((2, 2, 2)),
            dma((2,)),
        ],
        compiler_params=pltpu.CompilerParams(
            collective_id=0, has_side_effects=True, vmem_limit_bytes=67043328
        ),
    )(
        counts, table, tokens, cotangent, gate_blocks, up_blocks, down_blocks,
    )
    return pl.pallas_call(
        finish_kernel, out_shape=shapes, in_specs=[VM] * 5, out_specs=(VM,) * 5,
    )(*results)


def solution(mesh):
    placed = (
        P("fsdp", None),
        P("fsdp", None),
        P("tensor", "fsdp", None, None),
        P("tensor", "fsdp", None, None),
        P("tensor", "fsdp", None, None),
        P("tensor", None),
        P("tensor", None),
        P("tensor", None),
        P(None, "tensor"),
    )
    return jax.shard_map(
        shards,
        mesh=mesh,
        in_specs=placed,
        out_specs=(
            P("fsdp", "tensor"),
            P("fsdp", "tensor"),
            P("tensor", "fsdp", None, None),
            P("tensor", "fsdp", None, None),
            P("tensor", "fsdp", None, None),
        ),
        check_vma=False,
    )
```

time: 608 us -> 120 us (0.20)
  waiting for transfers between devices: 425 us -> 0 us
  Pallas kernels: 0 us -> 119 us
  other arithmetic: 78.8 us -> 0 us
  local copies, waits for them, and re-layouts: 45.1 us -> 0 us
  matrix products: 42 us -> 0 us
  between operations: 14.4 us -> 0.64 us
    reduce_scatter x5 -> x0, waiting for transfers between devices: 302 us -> none  [the longest x1 96.3 us: shards(): lax.psum_scatter(up_part[None].astype(jnp.bfloat16), 'fsdp', scatter_dime...]
    all_gather x3 -> x0, waiting for transfers between devices: 121 us -> none  [the longest x1 41.1 us: shards(): lax.all_gather(up_blocks, 'fsdp', axis=1, tiled=True)]
    pallas_call x0 -> x3, Pallas kernels: none -> 119 us  [the longest x1 115 us: shards(): pl.pallas_call(layer_kernel, out_shape=shapes, in_specs=[SM, SM] + [ANY]...]
    scatter-add x6 -> x0, other arithmetic: 67.3 us -> none  [collect(): return jax.ops.segment_sum(block_terms, segment_ids, num_segments=segments)]
    dot_general x9 -> x0, matrix products: 42 us -> none  [blockwise(): jnp.einsum(pattern, left_side, right_side, preferred_element_type=jnp.flo...]
    gather x6 -> x0, local copies, waits for them, and re-layouts: 14.5 us -> none  [the longest x1 3.31 us: shards(): hidden_sel = jnp.take(hidden, down_ff, axis=0)]
    unnamed x30 -> x0, local copies, waits for them, and re-layouts: 14.4 us -> none
    convert_element_type x4 -> x0, other arithmetic: 11.4 us -> none  [the longest x1 5.75 us: shards(): input_term.astype(jnp.bfloat16)]
  transfers between devices with their start and end apart: 8 -> 0, of which waited for: 7 -> 0; matrix products, arithmetic and copies ran while one was open for 19% -> 0% of each run, Pallas kernels for 0% -> 0%
where the time goes in v1:
time: 120 us
  Pallas kernels  119 us (99%)
    pallas_call x1, Pallas kernels, shards(): pl.pallas_call(layer_kernel, out_shape=shapes, in_specs=[SM, SM] + [ANY]...  115 us

profile of v1, /device:TPU:1, one launch (start us, length us, event | category | flops | bytes accessed | tf_op | source)
XLA Modules:
  0.0 119.8 jit_solution(16996317800613665207)
XLA Ops:
  0.6 2.1 %shard_map.128.tab = s32[26,128]{1,0:T(8,128)} custom-call(s32[3]{0:T(128)} %bitcast.1, s32[1,64]{1,0:T(1,128)} %gw.1, s32[1,64]{1,0:T(1,128)} %uw.1, s32[1,64]{1,0:T(1,128)} %dw.1), custom_call_target="tpu_custom_call" | custom-call | tf_op jit(solution)/shard_map/pallas_call | solution.py:530
  2.8 115.2 %shard_map.129 = (bf16[128,1024]{1,0:T(8,128)(2,1)}, bf16[128,1024]{1,0:T(8,128)(2,1)}, bf16[1,2,128,128]{3,2,1,0:T(8,128)(2,1)}, bf16[1,2,128,128]{3,2,1,0:T(8,128)(2,1)}, bf16[1,2,128,128]{3,2,1,0:T(8,128)(2,1)}) custom-call(s32[3]{0:T(128)} %bitcast.2, s32[26,128]{1,0:T(8,128)} %shard_map.128.tab, bf16[128,8192]{1,0:T(8,128)(2,1)} %x_hbm.1, ...), custom_call_target="tpu_custom_call" | custom-call | tf_op jit(solution)/shard_map/pallas_call | solution.py:536
  117.9 1.9 %shard_map.130 = (bf16[128,1024]{1,0:T(8,128)(2,1)}, bf16[128,1024]{1,0:T(8,128)(2,1)}, bf16[1,2,128,128]{3,2,1,0:T(8,128)(2,1)}, bf16[1,2,128,128]{3,2,1,0:T(8,128)(2,1)}, bf16[1,2,128,128]{3,2,1,0:T(8,128)(2,1)}) custom-call(bf16[128,1024]{1,0:T(8,128)(2,1)} %get-tuple-element.10.refs_0_, bf16[128,1024]{1,0:T(8,128)(2,1)} %get-tuple-element.11.refs_1_, ...), custom_call_target="tpu_custom_call" | custom-call | tf_op jit(solution)/shard_map/pallas_call | solution.py:584

commit v2 on v1

--- a/solution.py
+++ b/solution.py
@@ -254,11 +254,14 @@
         for k, j in chunks:
             products(me.fs(k, j), fl)
 
-    def theirs(chunks, fl):
+    def wait_theirs(chunks, fl):
         for k, j in chunks:
-            f = me.twin[k][j]
             for h in (0, 1):
-                arrive(w.at[half(fl, h, f * 6)], rp.at[fl, k, j, h])
+                arrive(w.at[half(fl, h, me.twin[k][j] * 6)], rp.at[fl, k, j, h])
+
+    def theirs(chunks, fl, wait=True):
+        if wait:
+            wait_theirs(chunks, fl)
         for k, j in chunks:
             products(me.twin[k][j], fl)
 
@@ -294,25 +297,32 @@
         return s[first + tab[END + kind, c]] * tab[SOME + kind, c].astype(F32)
 
     begin(0)
+    begin(1)
+    take(1, 0)
     arrive(x, lsem.at[3])
-    arrive(g, lsem.at[4])
-    mine(groups[0], 0)
-    for i in range(1, 7):
-        take(i, 0)
-        if i == 4:
-            begin(1)
-        mine(groups[i], 0)
-        theirs(groups[i - 1], 0)
-    mine(groups[0], 1)
+    mine(groups[0] + groups[1], 0)
+    take(2, 0)
     take(1, 1)
-    theirs(groups[6], 0)
+    theirs(groups[0], 0)
+    mine(groups[2], 0)
+    take(3, 0)
+    take(2, 1)
+    theirs(groups[1], 0)
+    mine(groups[3], 0)
+    take(4, 0)
+    theirs(groups[2], 0)
+    mine(groups[4], 0)
+    take(5, 0)
+    take(3, 1)
+    theirs(groups[3], 0)
+    mine(groups[5], 0)
+    take(6, 0)
+    theirs(groups[4], 0)
+    mine(groups[6], 0)
+    take(4, 1)
+    theirs(groups[5] + groups[6], 0)
     run(GATE, SLOTS, 0, lambda n: p[n])
-    take(2, 1)
-    take(3, 1)
     run(UP, SLOTS, SLOTS, lambda n: p[SLOTS + n])
-    mine(groups[1], 1)
-    theirs(groups[0], 1)
-    take(4, 1)
 
     def act(c, _):
         gate = pick(0, GATE, c)
@@ -326,43 +336,44 @@
 
     lax.fori_loop(0, cols, act, 0)
     take(5, 1)
-    mine(groups[2] + groups[3], 1)
-    theirs(groups[1], 1)
+    arrive(g, lsem.at[4])
+    mine(groups[0] + groups[1] + groups[2], 1)
     take(6, 1)
-    mine(groups[4] + groups[5] + groups[6], 1)
-    theirs(groups[2] + groups[3], 1)
-    theirs(groups[4] + groups[5] + groups[6], 1)
-
-    def opiece(a, zl, m):
-        return o.at[a, zl * 4 + me.xs[m % 4]]
+    wait_theirs(sum(groups, ()), 1)
+
+    def opiece(b, zl, m):
+        return o.at[b, zl * 4 + me.xs[m % 4]]
 
     def put(a, first, kind):
         def body(q, _):
             for r in range(8):
-                o[a, q, :, r * BK : (r + 1) * BK] = pick(first, kind, q * 8 + r).astype(BF)
+                at = slice(r % 4 * BK, (r % 4 + 1) * BK)
+                o[2 * a + r // 4, q, :, at] = pick(first, kind, q * 8 + r).astype(BF)
             return 0
 
         lax.fori_loop(0, 8, body, 0)
 
     def x_start(a):
-        send(opiece(a, 0, 2), x2.at[a, 0], rx2.at[a, 0], me.tdev(1))
-        send(opiece(a, 1, 2), x2.at[a, 1], rx2.at[a, 1], me.tdev(-1))
-        send(opiece(a, 1, 1), xr.at[a, 0, 1], rxr.at[a, 0, 1], me.tdev(1))
-        send(opiece(a, 0, -1), xr.at[a, 1, 0], rxr.at[a, 1, 0], me.tdev(-1))
-
-    def x_pass(a):
+        for b in (2 * a, 2 * a + 1):
+            send(opiece(b, 0, 2), x2.at[b, 0], rx2.at[b, 0], me.tdev(1))
+            send(opiece(b, 1, 2), x2.at[b, 1], rx2.at[b, 1], me.tdev(-1))
+        for b in (2 * a, 2 * a + 1):
+            send(opiece(b, 1, 1), xr.at[b, 0, 1], rxr.at[b, 0, 1], me.tdev(1))
+            send(opiece(b, 0, -1), xr.at[b, 1, 0], rxr.at[b, 1, 0], me.tdev(-1))
+
+    def x_pass(b):
         for h, m in ((0, 1), (1, -1)):
-            arrive(x2.at[a, h], rx2.at[a, h])
-            x2[a, h] = add2(o[a, h * 4 + me.xs[m % 4]], x2[a, h])
-            send(x2.at[a, h], xr.at[a, h, h], rxr.at[a, h, h], me.tdev(m))
-
-    def x_end(a):
+            arrive(x2.at[b, h], rx2.at[b, h])
+            x2[b, h] = add2(o[b, h * 4 + me.xs[m % 4]], x2[b, h])
+            send(x2.at[b, h], xr.at[b, h, h], rxr.at[b, h, h], me.tdev(m))
+
+    def x_end(b):
         for e in (0, 1):
             for h in (0, 1):
-                arrive(xr.at[a, e, h], rxr.at[a, e, h])
+                arrive(xr.at[b, e, h], rxr.at[b, e, h])
         other = 1 - me.zl
-        tz[a] = add3(o[a, me.across], xr[a, 0, other], xr[a, 1, other]).astype(BF)
-        send(tz.at[a], zlb.at[a], rl.at[a], me.tdev(flip=True))
+        tz[b] = add3(o[b, me.across], xr[b, 0, other], xr[b, 1, other]).astype(BF)
+        send(tz.at[b], zlb.at[b], rl.at[b], me.tdev(flip=True))
 
     results = []
 
@@ -371,11 +382,11 @@
         copy.start()
         results.append(copy)
 
-    def l_end(a):
-        own_sum = add3(o[a, me.line[0]], xr[a, 0, me.zl], xr[a, 1, me.zl])
-        arrive(zlb.at[a], rl.at[a])
-        fin[a] = (own_sum + zlb[a].astype(F32)).astype(BF)
-        result(fin.at[a], (out_hbm, ing_hbm)[a])
+    def l_end(b):
+        own_sum = add3(o[b, me.line[0]], xr[b, 0, me.zl], xr[b, 1, me.zl])
+        arrive(zlb.at[b], rl.at[b])
+        fin[b] = (own_sum + zlb[b].astype(F32)).astype(BF)
+        result(fin.at[b], (out_hbm, ing_hbm)[b // 2].at[:, pl.ds(b % 2 * 512, 512)])
 
     def core_send(k, fl):
         for j in (2, 1, 3, 0):
@@ -437,30 +448,35 @@
     def live(k, n):
         return (n < cnt[k]).astype(F32)
 
-    def down_grads(f, _):
-        for slot in (0, 1):
-            n = 2 * f + slot
-            d[f, 4 + slot] = (dot_tn(hid[tab[DF, n]], g[tab[DD, n]]) * live(2, n)).astype(BF)
+    def down_grads(i, _):
+        for e in range(4):
+            f = i * 4 + e
+            for slot in (0, 1):
+                n = 2 * f + slot
+                d[f, 4 + slot] = (dot_tn(hid[tab[DF, n]], g[tab[DD, n]]) * live(2, n)).astype(BF)
         return 0
 
     def in_grads(k):
         def body(i, _):
-            f = me.zs[k] * 8 + i
-            for slot in (0, 1):
-                n = 2 * f + slot
-                d[f, slot] = (dot_tn(x[tab[GR, n]], delta[tab[GC, n]]) * live(0, n)).astype(BF)
-                d[f, 2 + slot] = (dot_tn(x[tab[UR, n]], delta[cols + tab[UC, n]]) * live(1, n)).astype(BF)
+            for e in (0, 1):
+                f = me.zs[k] * 8 + i * 2 + e
+                for slot in (0, 1):
+                    n = 2 * f + slot
+                    d[f, slot] = (dot_tn(x[tab[GR, n]], delta[tab[GC, n]]) * live(0, n)).astype(BF)
+                    d[f, 2 + slot] = (dot_tn(x[tab[UR, n]], delta[cols + tab[UC, n]]) * live(1, n)).astype(BF)
             return 0
 
-        lax.fori_loop(0, 8, body, 0)
+        lax.fori_loop(0, 4, body, 0)
         core_send(k, 0)
 
     run(OUT, SLOTS, 0, lambda v: dot_nn(hid[v & 63], w[v >> 6]))
     put(0, 0, OUT)
     x_start(0)
-    lax.fori_loop(0, 32, down_grads, 0)
+    lax.fori_loop(0, 8, down_grads, 0)
     for k in (2, 1, 3, 0):
         core_send(k, 1)
+    mine(groups[3] + groups[4] + groups[5] + groups[6], 1)
+    theirs(sum(groups, ()), 1, wait=False)
     run(HID, SLOTS, 2 * SLOTS, lambda n: p[2 * SLOTS + n])
 
     def act_grad(c, _):
@@ -472,39 +488,45 @@
     lax.fori_loop(0, cols, act_grad, 0)
     for k in (2, 1, 3, 0):
         y_start(k, 1)
+    in_grads(2)
+    in_grads(1)
+    x_pass(0)
+    x_pass(1)
+    for k in (2, 1, 3, 0):
+        y_pass(k, 1)
     run(INP, 2 * SLOTS, SLOTS, lambda v: dot_nt(delta[v & 63], w[v >> 6]))
     put(1, SLOTS, INP)
     x_start(1)
-    in_grads(2)
-    x_pass(0)
-    in_grads(1)
     y_start(2, 0)
     in_grads(3)
     y_start(1, 0)
     in_grads(0)
     y_start(3, 0)
     for k in (2, 1, 3, 0):
-        y_pass(k, 1)
+        y_end(k, 1)
     y_start(0, 0)
-    for k in (2, 1, 3, 0):
-        y_end(k, 1)
+    x_end(0)
     y_pass(2, 0)
+    x_end(1)
     z_pass(1)
-    x_end(0)
     y_pass(1, 0)
+    x_pass(2)
     y_pass(3, 0)
     y_end(2, 0)
-    x_pass(1)
+    x_pass(3)
     y_pass(0, 0)
     y_end(1, 0)
+    y_end(3, 0)
+    l_end(0)
+    l_end(1)
     z_end(1)
-    l_end(0)
-    y_end(3, 0)
     z_pass(0)
     y_end(0, 0)
-    x_end(1)
+    x_end(2)
+    x_end(3)
     z_end(0)
-    l_end(1)
+    l_end(2)
+    l_end(3)
     for copy in results:
         copy.wait()
     send.finish()
@@ -546,7 +568,7 @@
             pltpu.VMEM((3 * SLOTS, BK, BK), F32),
             pltpu.VMEM((cols, BK, BK), BF),
             pltpu.VMEM((2 * cols, BK, BK), BF),
-            pltpu.VMEM((2, 8, toks, 1024), BF),
+            pltpu.VMEM((4, 8, toks, 512), BF),
             pltpu.VMEM((32, 6, BK, BK), BF),
             pltpu.VMEM((4, 4, 6, BK, BK), BF),
             pltpu.VMEM((4, 6, BK, BK), BF),
@@ -554,15 +576,15 @@
             pltpu.VMEM((4, 6, BK, BK), BF),
             pltpu.VMEM((6, BK, BK), BF),
             pltpu.VMEM((2, 6, BK, BK), BF),
-            pltpu.VMEM((2, 2, toks, 1024), BF),
-            pltpu.VMEM((2, 2, 2, toks, 1024), BF),
-            pltpu.VMEM((2, toks, 1024), BF),
-            pltpu.VMEM((2, toks, 1024), BF),
-            pltpu.VMEM((2, toks, 1024), BF),
+            pltpu.VMEM((4, 2, toks, 512), BF),
+            pltpu.VMEM((4, 2, 2, toks, 512), BF),
+            pltpu.VMEM((4, toks, 512), BF),
+            pltpu.VMEM((4, toks, 512), BF),
+            pltpu.VMEM((4, toks, 512), BF),
             pltpu.VMEM((6, BK, BK), BF),
             dma((5,)),
-            dma((5,)),
-            dma((240,)),
+            dma((7,)),
+            dma((256,)),
             dma((2, 4, 2)),
             dma((2, 4, 4, 2)),
             dma((2, 4, 4, 2)),
@@ -571,9 +593,9 @@
             dma((2, 4, 2, 2)),
             dma((2, 2)),
             dma((2, 2, 2)),
-            dma((2, 2)),
-            dma((2, 2, 2)),
-            dma((2,)),
+            dma((4, 2)),
+            dma((4, 2, 2)),
+            dma((4,)),
         ],
         compiler_params=pltpu.CompilerParams(
             collective_id=0, has_side_effects=True, vmem_limit_bytes=67043328

time: 120 us -> 107 us (0.89)
  Pallas kernels: 119 us -> 106 us
    pallas_call x1, Pallas kernels: 115 us -> 102 us  [shards(): pl.pallas_call(layer_kernel, out_shape=shapes, in_specs=[SM, SM] + [ANY]...]
where the time goes in v2:
time: 107 us; the launch traced here: 106 us
  Pallas kernels  106 us (99%)
    pallas_call x1, Pallas kernels, shards(): pl.pallas_call(layer_kernel, out_shape=shapes, in_specs=[SM, SM] + [ANY]...  102 us

profile of v2, /device:TPU:1, one launch (start us, length us, event | category | flops | bytes accessed | tf_op | source)
XLA Modules:
  0.0 106.4 jit_solution(2277060302706090893)
XLA Ops:
  0.6 2.1 %shard_map.128.tab = s32[26,128]{1,0:T(8,128)} custom-call(s32[3]{0:T(128)} %bitcast.1, s32[1,64]{1,0:T(1,128)} %gw.1, s32[1,64]{1,0:T(1,128)} %uw.1, s32[1,64]{1,0:T(1,128)} %dw.1), custom_call_target="tpu_custom_call" | custom-call | tf_op jit(solution)/shard_map/pallas_call | solution.py:552
  2.8 101.7 %shard_map.129 = (bf16[128,1024]{1,0:T(8,128)(2,1)}, bf16[128,1024]{1,0:T(8,128)(2,1)}, bf16[1,2,128,128]{3,2,1,0:T(8,128)(2,1)}, bf16[1,2,128,128]{3,2,1,0:T(8,128)(2,1)}, bf16[1,2,128,128]{3,2,1,0:T(8,128)(2,1)}) custom-call(s32[3]{0:T(128)} %bitcast.2, s32[26,128]{1,0:T(8,128)} %shard_map.128.tab, bf16[128,8192]{1,0:T(8,128)(2,1)} %x_hbm.1, ...), custom_call_target="tpu_custom_call" | custom-call | tf_op jit(solution)/shard_map/pallas_call | solution.py:558
  104.5 1.9 %shard_map.130 = (bf16[128,1024]{1,0:T(8,128)(2,1)}, bf16[128,1024]{1,0:T(8,128)(2,1)}, bf16[1,2,128,128]{3,2,1,0:T(8,128)(2,1)}, bf16[1,2,128,128]{3,2,1,0:T(8,128)(2,1)}, bf16[1,2,128,128]{3,2,1,0:T(8,128)(2,1)}) custom-call(bf16[128,1024]{1,0:T(8,128)(2,1)} %get-tuple-element.10.refs_0_, bf16[128,1024]{1,0:T(8,128)(2,1)} %get-tuple-element.11.refs_1_, ...), custom_call_target="tpu_custom_call" | custom-call | tf_op jit(solution)/shard_map/pallas_call | solution.py:606

commit v3 on v2

--- a/solution.py
+++ b/solution.py
@@ -71,11 +71,11 @@
     pltpu.make_async_copy(ref, ref, sem).wait()
 
 
-def meet(devs):
+def greet(devs):
     barrier = pltpu.get_barrier_semaphore()
     for dev in devs:
         pl.semaphore_signal(barrier, inc=1, device_id=dev, device_id_type=MESH)
-    pl.semaphore_wait(barrier, len(devs))
+    return lambda: pl.semaphore_wait(barrier, len(devs))
 
 
 ORDER, KEEP, END, SOME = 0, 5, 10, 15
@@ -113,7 +113,7 @@
     return q, v - q * 14
 
 
-def table_kernel(counts, gw, uw, dw, tab):
+def make_table(counts, gw, uw, dw, tab):
     n64 = lax.broadcasted_iota(jnp.int32, (1, SLOTS), 1)
     gr, gc = split14(gw[...])
     ur, uc = split14(uw[...])
@@ -172,15 +172,17 @@
 
 
 def layer_kernel(
-    cnt, tab, x_hbm, g_hbm, gate_hbm, up_hbm, down_hbm,
+    cnt, gwv, uwv, dwv, x_hbm, g_hbm, gate_hbm, up_hbm, down_hbm,
     out_hbm, ing_hbm, gg_hbm, ug_hbm, dg_hbm,
-    x, g, w, p, s, hid, delta,
+    x, g, w, p, s, hid, delta, tabv, tab,
     o, d, pbuf, y2, yr, bbuf, z2, zr, x2, xr, tz, zlb, fin, fing,
-    lsem, fsem, ssem, rz, ry, rp, rq, ry2, ryr, rz2, rzr, rx2, rxr, rl,
+    lsem, tsem, fsem, ssem, rz, ry, rp, rq, ry2, ryr, rz2, rzr, rx2, rxr, rl,
 ):
     me = Place()
     own = me.fs()
     cols = hid.shape[0]
+    met = greet([me.dev(1), me.dev(3), me.dev(0, 1), me.dev(0, 3), me.dev(flip=True),
+                 me.tdev(1), me.tdev(3), me.tdev(flip=True)])
     local = [
         pltpu.make_async_copy(src.at[0], w.at[pl.ds(own * 6 + 2 * i, 2)], lsem.at[i])
         for i, src in enumerate((gate_hbm, up_hbm, down_hbm))
@@ -195,8 +197,7 @@
         return 0
 
     lax.fori_loop(0, x.shape[0], bring, 0)
-    meet([me.dev(1), me.dev(3), me.dev(0, 1), me.dev(0, 3), me.dev(flip=True),
-          me.tdev(1), me.tdev(3), me.tdev(flip=True)])
+    met()
     for copy in local:
         copy.wait()
     send = Sender(ssem)
@@ -213,25 +214,23 @@
     def to_core(k, j, fl, h):
         send(piece(k, j, fl, h), piece(k, j, fl, h), rp.at[fl, k, j, h], me.dev(flip=True))
 
-    def on_y(k, j, fl):
-        for h in (0, 1):
-            arrive(piece(k, j, fl, h), ry.at[fl, k, j, h])
-            if j == 3 and h == 0:
-                to_y(k, j, fl, h, 1)
-            if j == 1 and h == 1:
-                to_y(k, j, fl, h, -1)
-            to_core(k, j, fl, h)
-
-    def on_z(k, fl):
-        for h in (0, 1):
-            arrive(piece(k, 0, fl, h), rz.at[fl, k, h])
-            if k == 3 and h == 0:
-                to_z(k, fl, h, 1)
-            if k == 1 and h == 1:
-                to_z(k, fl, h, -1)
-            to_y(k, 0, fl, h, 1)
-            to_y(k, 0, fl, h, -1)
-            to_core(k, 0, fl, h)
+    def on_y(k, j, fl, h):
+        arrive(piece(k, j, fl, h), ry.at[fl, k, j, h])
+        if j == 3 and h == 0:
+            to_y(k, j, fl, h, 1)
+        if j == 1 and h == 1:
+            to_y(k, j, fl, h, -1)
+        to_core(k, j, fl, h)
+
+    def on_z(k, fl, h):
+        arrive(piece(k, 0, fl, h), rz.at[fl, k, h])
+        if k == 3 and h == 0:
+            to_z(k, fl, h, 1)
+        if k == 1 and h == 1:
+            to_z(k, fl, h, -1)
+        to_y(k, 0, fl, h, 1)
+        to_y(k, 0, fl, h, -1)
+        to_core(k, 0, fl, h)
 
     def begin(fl):
         for h in (0, 1):
@@ -276,29 +275,34 @@
     )
 
     def take(i, fl):
-        for k, j in groups[i]:
-            if j == 0:
-                on_z(k, fl)
-            else:
-                on_y(k, j, fl)
-
-    def run(kind, count, first, term):
+        for h in (0, 1):
+            for k, j in groups[i]:
+                if j == 0:
+                    on_z(k, fl, h)
+                else:
+                    on_y(k, j, fl, h)
+
+    def run(kind, count, first, term, wide=UNROLL):
         def body(step, acc):
-            for u in range(UNROLL):
-                i = step * UNROLL + u
+            for u in range(wide):
+                i = step * wide + u
                 keep = tab[KEEP + kind, i].astype(F32)
                 acc = acc * keep + term(tab[ORDER + kind, i])
                 s[first + i] = acc
             return acc
 
-        lax.fori_loop(0, count // UNROLL, body, jnp.zeros((BK, BK), F32))
+        lax.fori_loop(0, count // wide, body, jnp.zeros((BK, BK), F32))
 
     def pick(first, kind, c):
         return s[first + tab[END + kind, c]] * tab[SOME + kind, c].astype(F32)
 
     begin(0)
     begin(1)
+    make_table(cnt, gwv, uwv, dwv, tabv)
+    table = pltpu.make_async_copy(tabv, tab, tsem)
+    table.start()
     take(1, 0)
+    table.wait()
     arrive(x, lsem.at[3])
     mine(groups[0] + groups[1], 0)
     take(2, 0)
@@ -341,6 +345,13 @@
     take(6, 1)
     wait_theirs(sum(groups, ()), 1)
 
+    results = []
+
+    def result(src, dst):
+        copy = pltpu.make_async_copy(src, dst, fsem.at[len(results)])
+        copy.start()
+        results.append(copy)
+
     def opiece(b, zl, m):
         return o.at[b, zl * 4 + me.xs[m % 4]]
 
@@ -353,11 +364,11 @@
 
         lax.fori_loop(0, 8, body, 0)
 
-    def x_start(a):
-        for b in (2 * a, 2 * a + 1):
+    def x_start(bs):
+        for b in bs:
             send(opiece(b, 0, 2), x2.at[b, 0], rx2.at[b, 0], me.tdev(1))
             send(opiece(b, 1, 2), x2.at[b, 1], rx2.at[b, 1], me.tdev(-1))
-        for b in (2 * a, 2 * a + 1):
+        for b in bs:
             send(opiece(b, 1, 1), xr.at[b, 0, 1], rxr.at[b, 0, 1], me.tdev(1))
             send(opiece(b, 0, -1), xr.at[b, 1, 0], rxr.at[b, 1, 0], me.tdev(-1))
 
@@ -374,13 +385,6 @@
         other = 1 - me.zl
         tz[b] = add3(o[b, me.across], xr[b, 0, other], xr[b, 1, other]).astype(BF)
         send(tz.at[b], zlb.at[b], rl.at[b], me.tdev(flip=True))
-
-    results = []
-
-    def result(src, dst):
-        copy = pltpu.make_async_copy(src, dst, fsem.at[len(results)])
-        copy.start()
-        results.append(copy)
 
     def l_end(b):
         own_sum = add3(o[b, me.line[0]], xr[b, 0, me.zl], xr[b, 1, me.zl])
@@ -469,63 +473,64 @@
         lax.fori_loop(0, 4, body, 0)
         core_send(k, 0)
 
-    run(OUT, SLOTS, 0, lambda v: dot_nn(hid[v & 63], w[v >> 6]))
+    def act_grad(c, _):
+        hg = pick(2 * SLOTS, HID, c)
+        delta[c] = (hg * p[c]).astype(BF)
+        delta[cols + c] = (hg * p[cols + c]).astype(BF)
+        return 0
+
+    run(OUT, SLOTS, 0, lambda v: dot_nn(hid[v & 63], w[v >> 6]), 16)
     put(0, 0, OUT)
-    x_start(0)
+    x_start((0, 1))
     lax.fori_loop(0, 8, down_grads, 0)
     for k in (2, 1, 3, 0):
         core_send(k, 1)
     mine(groups[3] + groups[4] + groups[5] + groups[6], 1)
     theirs(sum(groups, ()), 1, wait=False)
+    y_start(2, 1)
+    y_start(1, 1)
     run(HID, SLOTS, 2 * SLOTS, lambda n: p[2 * SLOTS + n])
-
-    def act_grad(c, _):
-        hg = pick(2 * SLOTS, HID, c)
-        delta[c] = (hg * p[c]).astype(BF)
-        delta[cols + c] = (hg * p[cols + c]).astype(BF)
-        return 0
-
     lax.fori_loop(0, cols, act_grad, 0)
-    for k in (2, 1, 3, 0):
-        y_start(k, 1)
+    y_start(3, 1)
+    y_start(0, 1)
     in_grads(2)
     in_grads(1)
     x_pass(0)
     x_pass(1)
     for k in (2, 1, 3, 0):
         y_pass(k, 1)
-    run(INP, 2 * SLOTS, SLOTS, lambda v: dot_nt(delta[v & 63], w[v >> 6]))
+    y_start(2, 0)
+    run(INP, 2 * SLOTS, SLOTS, lambda v: dot_nt(delta[v & 63], w[v >> 6]), 16)
     put(1, SLOTS, INP)
-    x_start(1)
-    y_start(2, 0)
+    x_start((2, 3))
+    y_start(1, 0)
     in_grads(3)
-    y_start(1, 0)
     in_grads(0)
     y_start(3, 0)
     for k in (2, 1, 3, 0):
         y_end(k, 1)
     y_start(0, 0)
+    y_pass(2, 0)
     x_end(0)
-    y_pass(2, 0)
     x_end(1)
+    y_pass(1, 0)
     z_pass(1)
-    y_pass(1, 0)
     x_pass(2)
+    x_pass(3)
     y_pass(3, 0)
     y_end(2, 0)
-    x_pass(3)
+    l_end(0)
+    l_end(1)
     y_pass(0, 0)
     y_end(1, 0)
     y_end(3, 0)
-    l_end(0)
-    l_end(1)
+    x_end(2)
+    z_pass(0)
     z_end(1)
-    z_pass(0)
     y_end(0, 0)
-    x_end(2)
     x_end(3)
+    l_end(2)
     z_end(0)
-    l_end(2)
     l_end(3)
     for copy in results:
         copy.wait()
@@ -549,16 +554,10 @@
         jax.ShapeDtypeStruct((1, 2, BK, BK), BF),
     )
     counts = block_counts.reshape(3)
-    table = pl.pallas_call(
-        table_kernel,
-        out_shape=jax.ShapeDtypeStruct((26, BK), jnp.int32),
-        in_specs=[SM, VM, VM, VM],
-        out_specs=VM,
-    )(counts, gate_where, up_where, down_where)
     results = pl.pallas_call(
         layer_kernel,
         out_shape=shapes,
-        in_specs=[SM, SM] + [ANY] * 5,
+        in_specs=[SM, VM, VM, VM] + [ANY] * 5,
         out_specs=(ANY,) * 5,
         scratch_shapes=[
             pltpu.VMEM((tokens.shape[1] // BK, toks, BK), BF),
@@ -568,6 +567,8 @@
             pltpu.VMEM((3 * SLOTS, BK, BK), F32),
             pltpu.VMEM((cols, BK, BK), BF),
             pltpu.VMEM((2 * cols, BK, BK), BF),
+            pltpu.VMEM((26, BK), jnp.int32),
+            pltpu.SMEM((26, BK), jnp.int32),
             pltpu.VMEM((4, 8, toks, 512), BF),
             pltpu.VMEM((32, 6, BK, BK), BF),
             pltpu.VMEM((4, 4, 6, BK, BK), BF),
@@ -583,6 +584,7 @@
             pltpu.VMEM((4, toks, 512), BF),
             pltpu.VMEM((6, BK, BK), BF),
             dma((5,)),
+            dma,
             dma((7,)),
             dma((256,)),
             dma((2, 4, 2)),
@@ -601,7 +603,7 @@
             collective_id=0, has_side_effects=True, vmem_limit_bytes=67043328
         ),
     )(
-        counts, table, tokens, cotangent, gate_blocks, up_blocks, down_blocks,
+        counts, gate_where, up_where, down_where, tokens, cotangent, gate_blocks, up_blocks, down_blocks,
     )
     return pl.pallas_call(
         finish_kernel, out_shape=shapes, in_specs=[VM] * 5, out_specs=(VM,) * 5,

time: 107 us -> 100 us (0.935)
  Pallas kernels: 106 us -> 99.6 us
    pallas_call x2 -> x1, Pallas kernels: 104 us -> 97.7 us  [shards(): pl.pallas_call(layer_kernel, out_shape=shapes, in_specs=[SM, VM, VM, VM]...]
where the time goes in v3:
time: 100 us
  Pallas kernels  99.6 us (100%)
    pallas_call x1, Pallas kernels, shards(): pl.pallas_call(layer_kernel, out_shape=shapes, in_specs=[SM, VM, VM, VM]...  97.7 us

profile of v3, /device:TPU:1, one launch (start us, length us, event | category | flops | bytes accessed | tf_op | source)
XLA Modules:
  0.0 100.3 jit_solution(17798152886738869976)
XLA Ops:
  0.6 97.7 %shard_map.128 = (bf16[128,1024]{1,0:T(8,128)(2,1)}, bf16[128,1024]{1,0:T(8,128)(2,1)}, bf16[1,2,128,128]{3,2,1,0:T(8,128)(2,1)}, bf16[1,2,128,128]{3,2,1,0:T(8,128)(2,1)}, bf16[1,2,128,128]{3,2,1,0:T(8,128)(2,1)}) custom-call(s32[3]{0:T(128)} %bitcast.1, s32[1,64]{1,0:T(1,128)} %gwv.1, s32[1,64]{1,0:T(1,128)} %uwv.1, s32[1,64]{1,0:T(1,128)} %dwv.1, ...), custom_call_target="tpu_custom_call" | custom-call | tf_op jit(solution)/shard_map/pallas_call | solution.py:557
  98.3 1.9 %shard_map.129 = (bf16[128,1024]{1,0:T(8,128)(2,1)}, bf16[128,1024]{1,0:T(8,128)(2,1)}, bf16[1,2,128,128]{3,2,1,0:T(8,128)(2,1)}, bf16[1,2,128,128]{3,2,1,0:T(8,128)(2,1)}, bf16[1,2,128,128]{3,2,1,0:T(8,128)(2,1)}) custom-call(bf16[128,1024]{1,0:T(8,128)(2,1)} %get-tuple-element.10.refs_0_, bf16[128,1024]{1,0:T(8,128)(2,1)} %get-tuple-element.11.refs_1_, ...), custom_call_target="tpu_custom_call" | custom-call | tf_op jit(solution)/shard_map/pallas_call | solution.py:608
